TPU v7x, 32 devices: a whole 2x2x4 slice. The times are simulated.
32 devices in a mesh: batch: 8 (over z, y), mp: 4 (over x, core).
Axes of the slice: x: 2, y: 2, z: 4, core: 2. Of those that a mesh axis runs over, the one named last changes fastest.
Arguments:
- lookup_ids: int32 [64, 16384], P('batch'), may hold values from 0 to 8191
- table_feature: int32 [64], replicated, may hold values from 0 to 63, each once
- tables: bfloat16 [64, 8192, 128], P('batch'), may hold values from -6 to 6
- cross_down: bfloat16 [2, 8192, 512], P(None, 'mp'), may hold values from -0.0625 to 0.0625
- cross_up: bfloat16 [2, 512, 8192], P(None, None, 'mp'), may hold values from -0.25 to 0.25
- cross_bias: float32 [2, 8192], P(None, 'mp'), may hold values from -3 to 3
Outputs:
- crossed: bfloat16 [16384, 8192], P('batch', 'mp')
Inputs may be any that keep to these rules, and one draw needn't show every extreme that they name: `table_feature`: each number appears once.
All inputs are finite; a program needn't handle non-finite values.
Results may differ from a plain program's by a relative error of at most 0.015.
Values may be sent and summed in bfloat16 or wider, within the bound.
A program may use at most 128 MiB of HBM per device.

v0:
```python
import jax
import jax.numpy as jnp
from jax import lax
from jax.sharding import PartitionSpec as P


def per_device(lookup_ids, table_feature, tables, cross_down, cross_up, cross_bias):
    slots_local = tables.shape[0]
    feats = table_feature.shape[0]
    sources = lax.axis_size("batch")
    groups = lax.axis_size("mp")
    examples_local = lookup_ids.shape[1] // sources
    share = examples_local // groups
    start = lax.axis_index("mp") * share
    by_owner = lookup_ids.reshape(slots_local, sources, examples_local)
    wanted = lax.dynamic_slice_in_dim(by_owner, start, share, 2)
    looked = jnp.stack(
        [
            jnp.take(tables[slot], wanted[slot].reshape(sources * share), axis=0)
            for slot in range(slots_local)
        ],
        axis=1,
    )
    looked = looked.reshape(sources, share, slots_local, tables.shape[2])
    received = lax.all_to_all(
        lax.all_to_all(looked, "batch", split_axis=0, concat_axis=0, tiled=True),
        "mp",
        split_axis=3,
        concat_axis=1,
        tiled=True,
    )
    emb_local = received.shape[3]
    unfolded = jnp.transpose(received, (1, 0, 2, 3)).reshape(examples_local, feats, emb_local)
    placing = (table_feature[:, None] == jnp.arange(feats, dtype=jnp.int32)[None, :]).astype(
        jnp.bfloat16
    )
    ordered = jnp.einsum("rse,sf->ref", unfolded, placing, preferred_element_type=jnp.float32)
    embedded = ordered.astype(jnp.bfloat16).reshape(examples_local, emb_local * feats)
    embedded_wide = embedded.astype(jnp.float32)
    state = embedded
    for layer in range(len(cross_down)):
        weight_down = cross_down[layer]
        term = jnp.dot(state, weight_down, preferred_element_type=jnp.float32)
        term = term.astype(jnp.bfloat16).astype(jnp.float32)
        low = lax.psum(term.astype(jnp.bfloat16), "mp")
        high = (
            jnp.dot(low, cross_up[layer], preferred_element_type=jnp.float32)
            + cross_bias[layer][None, :]
        )
        state = (embedded_wide * high + state.astype(jnp.float32)).astype(jnp.bfloat16)
    return state


def solution(mesh):
    return jax.shard_map(
        per_device,
        mesh=mesh,
        in_specs=(
            P("batch", None),
            P(),
            P("batch", None, None),
            P(None, "mp", None),
            P(None, None, "mp"),
            P(None, "mp"),
        ),
        out_specs=P("batch", "mp"),
        check_vma=False,
    )
```

profile of v0, /device:TPU:0, one launch (start us, length us, event | category | flops | bytes accessed | tf_op | source)
XLA Modules:
  0.0 718.1 jit_solution(7940920189103681202)
XLA Ops:
  6.5 2.1 constant_dynamic-slice_fusion.7
  8.9 11.4 %slice_bitcast_fusion = (bf16[8192,128]{1,0:T(8,128)(2,1)}, bf16[8192,128]{1,0:T(8,128)(2,1)}, bf16[8192,128]{1,0:T(8,128)(2,1)}, bf16[8192,128]{1,0:T(8,128)(2,...) fusion(bf16[8,8192,128]{2,1,0:T(8,128)(2,1)} %param.10), kind=kLoop, calls=%fused_computation.27 | loop fusion | bytes 33554432 | tf_op jit(solution)/shard_map/squeeze | solution.py:19
  20.4 12.9 %gather_fusion.1 = bf16[4096,128]{1,0:T(8,128)(2,1)S(1)} fusion(bf16[8192,128]{1,0:T(8,128)(2,1)} %get-tuple-element.11, s32[4096]{0:T(1024)S(1)} %fusion.21), kind=kCustom, calls=%fused_computation.1.clone | custom fusion | bytes 2113536 | tf_op jit(solution)/shard_map/jit(_take)/gather | solution.py:19
  33.3 2.9 broadcast_select_fusion.6
  36.2 6.0 copy.42
  42.1 12.9 %gather_fusion.2 = bf16[4096,128]{1,0:T(8,128)(2,1)S(1)} fusion(bf16[8192,128]{1,0:T(8,128)(2,1)} %get-tuple-element.10, s32[4096]{0:T(1024)S(1)} %fusion.22), kind=kCustom, calls=%fused_computation.2.clone | custom fusion | bytes 2113536 | tf_op jit(solution)/shard_map/jit(_take)/gather | solution.py:19
  55.0 2.9 broadcast_select_fusion.5
  57.9 5.9 copy.43
  63.9 12.9 %gather_fusion.3 = bf16[4096,128]{1,0:T(8,128)(2,1)S(1)} fusion(bf16[8192,128]{1,0:T(8,128)(2,1)} %get-tuple-element.9, s32[4096]{0:T(1024)S(1)} %fusion.23), kind=kCustom, calls=%fused_computation.3.clone | custom fusion | bytes 2113536 | tf_op jit(solution)/shard_map/jit(_take)/gather | solution.py:19
  76.8 2.9 broadcast_select_fusion.4
  79.7 6.0 copy.44
  85.7 12.9 %gather_fusion.4 = bf16[4096,128]{1,0:T(8,128)(2,1)S(1)} fusion(bf16[8192,128]{1,0:T(8,128)(2,1)} %get-tuple-element.8, s32[4096]{0:T(1024)S(1)} %fusion.24), kind=kCustom, calls=%fused_computation.4.clone | custom fusion | bytes 2113536 | tf_op jit(solution)/shard_map/jit(_take)/gather | solution.py:19
  98.6 2.9 broadcast_select_fusion.3
  101.5 6.0 copy.45
  107.5 12.9 %gather_fusion.5 = bf16[4096,128]{1,0:T(8,128)(2,1)S(1)} fusion(bf16[8192,128]{1,0:T(8,128)(2,1)} %get-tuple-element.7, s32[4096]{0:T(1024)S(1)} %fusion.25), kind=kCustom, calls=%fused_computation.5.clone | custom fusion | bytes 2113536 | tf_op jit(solution)/shard_map/jit(_take)/gather | solution.py:19
  120.4 2.9 broadcast_select_fusion.2
  123.3 6.0 copy.46
  129.3 12.9 %gather_fusion.6 = bf16[4096,128]{1,0:T(8,128)(2,1)S(1)} fusion(bf16[8192,128]{1,0:T(8,128)(2,1)} %get-tuple-element.13, s32[4096]{0:T(1024)S(1)} %fusion.26), kind=kCustom, calls=%fused_computation.6.clone | custom fusion | bytes 2113536 | tf_op jit(solution)/shard_map/jit(_take)/gather | solution.py:19
  142.2 2.9 broadcast_select_fusion.1
  145.1 5.9 copy.47
  151.1 12.9 %gather_fusion.7 = bf16[4096,128]{1,0:T(8,128)(2,1)S(1)} fusion(bf16[8192,128]{1,0:T(8,128)(2,1)} %get-tuple-element.6, s32[4096]{0:T(1024)S(1)} %fusion.27), kind=kCustom, calls=%fused_computation.7.clone | custom fusion | bytes 2113536 | tf_op jit(solution)/shard_map/jit(_take)/gather | solution.py:19
  164.0 2.9 broadcast_select_fusion
  166.8 6.0 copy.48
  172.8 12.1 %gather_fusion = bf16[4096,128]{1,0:T(8,128)(2,1)S(1)} fusion(bf16[8192,128]{1,0:T(8,128)(2,1)S(1)} %get-tuple-element.12, s32[4096]{0:T(1024)S(1)} %fusion.20), kind=kCustom, calls=%fused_computation.clone | custom fusion | bytes 2113536 | tf_op jit(solution)/shard_map/jit(_take)/gather | solution.py:19
  184.9 0.0 copy-start.1
  185.0 2.9 broadcast_select_fusion.7
  187.8 5.9 copy.41
  193.8 42.8 %stack.35 = bf16[8,512,8,128]{1,2,3,0:T(8,128)(2,1)} concatenate(bf16[8,512,1,128]{1,2,3,0:T(2,128)(2,1)} %copy.41, bf16[8,512,1,128]{1,2,3,0:T(2,128)(2,1)S(1)} %copy-done.1, bf16[8,512,1,128]{1,2,3,0:T(2,128)(2,1)} %copy.43, bf16[8,512,1,128]{1,2,3,0:T(2,128)(2,1)} %copy.44, bf16[8,512,1,128]{1,2,3,0:T(2,128)(2,1)} %copy.45, bf16[8,512,1,128]{1,2,3,0:T(2,128)(2,1)} %copy.46, ...), dimensions={2} | concatenate | bytes 16777216 | tf_op jit(solution)/shard_map/stack | solution.py:17
  236.5 190.6 %all_to_all.23 = bf16[8,512,8,128]{1,2,3,0:T(8,128)(2,1)} all-to-all(bf16[8,512,8,128]{1,2,3,0:T(8,128)(2,1)} %stack.35), channel_id=1, replica_groups=mesh['batch'=8,'mp'=4] {'batch'}, dimensions={0} | all-to-all | bytes 16777216 | tf_op jit(solution)/shard_map/all_to_all | solution.py:26
  427.2 8.1 %copy.49 = bf16[8,512,8,128]{1,2,0,3:T(8,128)(2,1)} copy(bf16[8,512,8,128]{1,2,3,0:T(8,128)(2,1)} %all_to_all.23) | data formatting | bytes 16777216 | tf_op jit(solution)/shard_map/all_to_all | solution.py:26
  435.2 97.2 %all_to_all.24 = bf16[8,512,8,128]{1,2,0,3:T(8,128)(2,1)S(1)} all-to-all(bf16[8,512,8,128]{1,2,0,3:T(8,128)(2,1)} %copy.49), channel_id=1, replica_groups=mesh['batch'=8,'mp'=4] {'mp'}, dimensions={3} | all-to-all | bytes 16777216 | tf_op jit(solution)/shard_map/all_to_all | solution.py:25
  532.4 7.3 %copy.51 = bf16[8,4,512,8,32]{2,1,4,3,0:T(4,128)(2,1)} copy(bf16[8,4,512,8,32]{2,3,0,4,1:T(8,128)(2,1)S(1)} %bitcast.69) | data formatting | bytes 16777216 | tf_op jit(solution)/shard_map/all_to_all | solution.py:25
  539.7 14.4 %all_to_all.20 = bf16[8,2048,8,32]{1,3,2,0:T(8,128)(2,1)} reshape(bf16[8,4,512,8,32]{2,1,4,3,0:T(4,128)(2,1)} %copy.51) | data formatting | bytes 16777216 | tf_op jit(solution)/shard_map/all_to_all | solution.py:25
  554.1 10.1 %fusion.6 = bf16[2048,32,64]{0,2,1:T(8,128)(2,1)S(1)} fusion(bf16[2048,8,8,32]{0,3,2,1:T(8,128)(2,1)} %bitcast.68, s32[64]{0:T(128)S(1)} %copy-done.3), kind=kOutput, calls=%fused_computation.16 | convolution fusion | flops 541069312 | bytes 16777472 | tf_op jit(solution)/shard_map/rse,sf->ref/dot_general | solution.py:37
  564.2 0.0 copy-start
  564.2 3.4 copy-done
  567.6 7.3 %convolution_convert_fusion.1 = bf16[2048,512]{1,0:T(8,128)(2,1)} fusion(bf16[2048,2048]{0,1:T(8,128)(2,1)S(1)} %bitcast.66, bf16[2,2048,512]{2,1,0:T(8,128)(2,1)} %param.11), kind=kOutput, calls=%fused_computation.18 | convolution fusion | flops 4296015872 | bytes 12582912 | tf_op jit(solution)/shard_map/dot_general | solution.py:43
  574.9 0.0 all-reduce.3.cloned.1.call-update
  575.0 0.0 all-reduce.5.cloned.1.call-start
  575.0 11.9 %copy.53 = bf16[2048,2048]{1,0:T(8,128)(2,1)} copy(bf16[2048,2048]{0,1:T(8,128)(2,1)} %bitcast.67) | data formatting | bytes 16777216 | tf_op jit(solution)/shard_map/reshape | solution.py:38
  586.9 37.6 %all-reduce.3.cloned.1.call-done = bf16[2048,512]{1,0:T(8,128)(2,1)} async-done(((bf16[2048,512]{1,0:T(8,128)(2,1)}), bf16[2048,512]{1,0:T(8,128)(2,1)}) %all-reduce.3.cloned.1.call-update) | async-done | bytes 2097168 | tf_op jit(solution)/shard_map/psum | solution.py:45
  624.5 9.9 %fusion.2 = bf16[2048,2048]{1,0:T(8,128)(2,1)S(1)} fusion(bf16[2048,2048]{1,0:T(8,128)(2,1)} %copy.53, f32[2048]{0:T(1024)S(1)} %bitcast.96, bf16[2048,512]{1,0:T(8,128)(2,1)} %all-reduce.3.cloned.1.call-done, bf16[2,512,2048]{2,1,0:T(8,128)(2,1)} %param.12), kind=kOutput, calls=%fused_computation.12 | convolution fusion | flops 4315938816 | bytes 20979712 | tf_op jit(solution)/shard_map/dot_general | solution.py:47
  634.4 0.0 copy-start.5
  634.4 3.4 copy-done.5
  637.8 5.9 convolution_convert_fusion
  643.8 0.0 all-reduce.5.cloned.1.call-update
  643.8 51.6 %all-reduce.5.cloned.1.call-done = bf16[2048,512]{1,0:T(8,128)(2,1)} async-done(((bf16[2048,512]{1,0:T(8,128)(2,1)}), bf16[2048,512]{1,0:T(8,128)(2,1)}) %all-reduce.5.cloned.1.call-update) | async-done | bytes 2097168 | tf_op jit(solution)/shard_map/psum | solution.py:45
  695.4 15.9 %fusion.1 = bf16[2048,2048]{1,0:T(8,128)(2,1)} fusion(bf16[2048,2048]{1,0:T(8,128)(2,1)} %copy.53, bf16[2048,2048]{1,0:T(8,128)(2,1)} %copy-done.5, f32[2048]{0:T(1024)S(1)} %bitcast.95, bf16[2048,512]{1,0:T(8,128)(2,1)} %all-reduce.5.cloned.1.call-done, bf16[2,512,2048]{2,1,0:T(8,128)(2,1)} %param.12), kind=kOutput, calls=%fused_computation.11 | convolution fusion | flops 4320133120 | bytes 29368320 | tf_op jit(solution)/shard_map/dot_general | solution.py:47
  (25 shorter events, 0.2 us)
Async XLA Ops:
  6.5 617.9 %all-reduce.3.cloned.1.call-start = ((), (), s32[]{:S(2)}) async-start(), calls=%async_computation.2 | async-start | bytes 4194304 | tf_op jit(solution)/shard_map/psum | solution.py:45
  184.9 8.8 %copy-start.1 = (bf16[8,512,1,128]{1,2,3,0:T(2,128)(2,1)S(1)}, bf16[8,512,1,128]{1,2,3,0:T(2,128)(2,1)}, u32[]{:S(2)}) copy-start(bf16[8,512,1,128]{1,2,3,0:T(2,128)(2,1)} %copy.42) | copy-start | bytes 3145732
  539.7 14.4 %copy-start.3 = (s32[64]{0:T(128)S(1)}, s32[64]{0:T(128)}, u32[]{:S(2)}) copy-start(s32[64]{0:T(128)} %param.9) | copy-start | bytes 772
  564.2 3.4 copy-start
  567.6 7.4 %copy-start.2 = (f32[2,2048]{1,0:T(2,128)S(1)}, f32[2,2048]{1,0:T(2,128)}, u32[]{:S(2)}) copy-start(f32[2,2048]{1,0:T(2,128)} %param.13) | copy-start | bytes 49156
  575.0 120.4 %all-reduce.5.cloned.1.call-start = ((), (), s32[]{:S(2)}) async-start(), calls=%async_computation.3 | async-start | bytes 4194304 | tf_op jit(solution)/shard_map/psum | solution.py:45
  624.5 13.3 %copy-start.4 = (bf16[2,2048,512]{2,1,0:T(8,128)(2,1)S(1)}, bf16[2,2048,512]{2,1,0:T(8,128)(2,1)}, u32[]{:S(2)}) copy-start(bf16[2,2048,512]{2,1,0:T(8,128)(2,1)} %param.11) | copy-start | bytes 12582916
  634.4 3.4 copy-start.5
Sparse Core Ops, SparseCore 0:
  575.1 49.3 all-reduce.2
  643.9 51.4 all-reduce.4
where the time goes:
time: 725 us; the launch traced here: 718 us
  blocking collectives  288 us (40%)
  local copies, waits for them, and re-layouts  255 us (35%)
  waiting for transfers between devices  89.2 us (12%)
  matrix products  49.2 us (7%)
  other arithmetic  23.4 us (3%)
  between operations  13.7 us (2%)
    all_to_all x1, blocking collectives, per_device(): lax.all_to_all(looked, 'batch', split_axis=0, concat_axis=0, tiled=True)  191 us
    gather x8, local copies, waits for them, and re-layouts, per_device(): jnp.take(tables[slot], wanted[slot].reshape(sources * share), axis=0)  102 us
    all_to_all x1, blocking collectives, per_device(): lax.all_to_all(lax.all_to_all(looked, 'batch', split_axis=0, concat_axis=...  97.2 us
    another operation x9, local copies, waits for them, and re-layouts, per_device(): jnp.stack([jnp.take(tables[slot], wanted[slot].reshape(sources * share),...  90.5 us
    psum x2, waiting for transfers between devices, per_device(): low = lax.psum(term.astype(jnp.bfloat16), 'mp')  89.2 us
    dot_general x2, matrix products, per_device(): jnp.dot(low, cross_up[layer], preferred_element_type=jnp.float32)  25.8 us
    select_n x8, other arithmetic, per_device(): jnp.take(tables[slot], wanted[slot].reshape(sources * share), axis=0)  23.3 us
    all_to_all x2, local copies, waits for them, and re-layouts, per_device(): lax.all_to_all(lax.all_to_all(looked, 'batch', split_axis=0, concat_axis=...  21.7 us
  transfers between devices with their start and end apart: 2, of which 2 were waited for; matrix products, arithmetic and copies ran while one was open for 2% of the time, Pallas kernels for 0%

commit v1 on v0

v1 whole, which is shorter than its diff:
```python
import functools

import jax
import jax.numpy as jnp
from jax import lax
from jax.experimental import pallas as pl
from jax.experimental.pallas import tpu as pltpu
from jax.sharding import PartitionSpec as P

MESH = pl.DeviceIdType.MESH
GROUP = 16


def gather_kernel(ids_ref, table_ref, out_ref, wide, rows):
    sources, groups, _, emb_local, share = out_ref.shape
    slot = pl.program_id(0)
    buckets = wide.shape[0]
    step = 256

    @pl.loop(0, buckets // step)
    def _(i):
        part = pl.ds(pl.multiple_of(i * step, step), step)
        wide[part, :] = table_ref[0, part, :].astype(jnp.float32)

    unroll = 32

    @pl.loop(0, sources)
    def _(dest):
        @pl.loop(0, share // unroll)
        def _(i):
            base = pl.multiple_of(i * unroll, unroll)
            for k in range(unroll):
                at = ids_ref[slot, dest * share + base + k]
                rows[pl.ds(base + k, 1), :] = wide[pl.ds(at, 1), :]

        turned = rows[...].T.astype(jnp.bfloat16)
        for m in range(groups):
            out_ref[dest, m, 0] = turned[m * emb_local : (m + 1) * emb_local]


def gather(wanted, tables, sources, groups, share):
    slots, buckets, emb = tables.shape
    emb_local = emb // groups
    return pl.pallas_call(
        gather_kernel,
        out_shape=jax.ShapeDtypeStruct((sources, groups, slots, emb_local, share), tables.dtype),
        grid_spec=pltpu.PrefetchScalarGridSpec(
            num_scalar_prefetch=1,
            grid=(slots,),
            in_specs=[pl.BlockSpec((1, buckets, emb), lambda s, ids: (s, 0, 0))],
            out_specs=pl.BlockSpec(
                (sources, groups, 1, emb_local, share), lambda s, ids: (0, 0, s, 0, 0)
            ),
            scratch_shapes=[
                pltpu.VMEM((buckets, emb), jnp.float32),
                pltpu.VMEM((share, emb), jnp.float32),
            ],
        ),
        compiler_params=pltpu.CompilerParams(vmem_limit_bytes=40 * 2**20),
        name="lookup",
    )(wanted, tables)


def partner(me, mask, size):
    other = me
    bit = 1
    while bit < size:
        if mask & bit:
            other = other + bit * (1 - 2 * ((me // bit) % 2))
        bit *= 2
    return other


def exchange_kernel(sources, groups, src_ref, dst_ref, send_sem, recv_sem, own_sem):
    b, m = lax.axis_index("batch"), lax.axis_index("mp")
    masks = [
        (x, y)
        for x in range(sources - 1, -1, -1)
        for y in range(groups - 1, -1, -1)
        if (x, y) != (0, 0)
    ]
    peers = [(partner(b, x, sources), partner(m, y, groups)) for x, y in masks]
    barrier = pltpu.get_barrier_semaphore()
    for peer in peers:
        pl.semaphore_signal(barrier, inc=1, device_id=peer, device_id_type=MESH)
    pl.semaphore_wait(barrier, len(peers))
    copies = []
    for k, peer in enumerate(peers):
        copy = pltpu.make_async_remote_copy(
            src_ref=src_ref.at[peer[0], peer[1]],
            dst_ref=dst_ref.at[b, m],
            send_sem=send_sem.at[k],
            recv_sem=recv_sem.at[k],
            device_id=peer,
            device_id_type=MESH,
        )
        copy.start()
        copies.append(copy)
    own = pltpu.make_async_copy(src_ref.at[b, m], dst_ref.at[b, m], own_sem)
    own.start()
    own.wait()
    for copy in copies:
        copy.wait()


def exchange(sent):
    sources, groups = sent.shape[:2]
    peers = sources * groups - 1
    return pl.pallas_call(
        functools.partial(exchange_kernel, sources, groups),
        out_shape=jax.ShapeDtypeStruct(sent.shape, sent.dtype),
        in_specs=[pl.BlockSpec(memory_space=pl.ANY)],
        out_specs=pl.BlockSpec(memory_space=pl.ANY),
        scratch_shapes=[
            pltpu.SemaphoreType.DMA((peers,)),
            pltpu.SemaphoreType.DMA((peers,)),
            pltpu.SemaphoreType.DMA,
        ],
        compiler_params=pltpu.CompilerParams(collective_id=0, has_side_effects=True),
        name="exchange",
    )(sent)


def place_kernel(x_ref, placing_ref, down_ref, emb_ref, term_ref, total):
    sources, _, slots, group, share = x_ref.shape
    j = pl.program_id(1)
    x = x_ref[...].reshape(sources * slots * group, share)
    emb = lax.dot_general(
        x, placing_ref[...], (((0,), (0,)), ((), ())), preferred_element_type=jnp.float32
    ).astype(jnp.bfloat16)
    emb_ref[...] = emb
    part = jnp.dot(emb, down_ref[0], preferred_element_type=jnp.float32)

    @pl.when(j == 0)
    def _():
        total[...] = part

    @pl.when(j > 0)
    def _():
        total[...] += part

    @pl.when(j == pl.num_programs(1) - 1)
    def _():
        term_ref[...] = total[...].astype(jnp.bfloat16)


def place(received, placing, cross_down):
    sources, groups, slots, emb_local, share = received.shape
    _, width, rank = cross_down.shape
    cols = sources * slots * GROUP
    return pl.pallas_call(
        place_kernel,
        out_shape=(
            jax.ShapeDtypeStruct((groups * share, width), jnp.bfloat16),
            jax.ShapeDtypeStruct((groups * share, rank), jnp.bfloat16),
        ),
        grid=(groups, emb_local // GROUP),
        in_specs=[
            pl.BlockSpec((sources, 1, slots, GROUP, share), lambda i, j: (0, i, 0, j, 0)),
            pl.BlockSpec((cols, cols), lambda i, j: (0, 0)),
            pl.BlockSpec((1, cols, rank), lambda i, j: (0, j, 0)),
        ],
        out_specs=(
            pl.BlockSpec((share, cols), lambda i, j: (i, j)),
            pl.BlockSpec((share, rank), lambda i, j: (i, 0)),
        ),
        scratch_shapes=[pltpu.VMEM((share, rank), jnp.float32)],
        compiler_params=pltpu.CompilerParams(vmem_limit_bytes=40 * 2**20),
        name="place",
    )(received, placing, cross_down)


def per_device(lookup_ids, table_feature, tables, cross_down, cross_up, cross_bias):
    slots_local = tables.shape[0]
    feats = table_feature.shape[0]
    sources = lax.axis_size("batch")
    groups = lax.axis_size("mp")
    examples_local = lookup_ids.shape[1] // sources
    share = examples_local // groups
    start = lax.axis_index("mp") * share
    by_owner = lookup_ids.reshape(slots_local, sources, examples_local)
    wanted = lax.dynamic_slice_in_dim(by_owner, start, share, 2)
    wanted = wanted.reshape(slots_local, sources * share)
    received = exchange(gather(wanted, tables, sources, groups, share))
    fits = table_feature[:, None] == jnp.arange(feats, dtype=jnp.int32)[None, :]
    same = jnp.arange(GROUP)[:, None] == jnp.arange(GROUP)[None, :]
    placing = (
        (fits[:, None, None, :] & same[None, :, :, None])
        .reshape(feats * GROUP, GROUP * feats)
        .astype(jnp.bfloat16)
    )
    embedded, term = place(received, placing, cross_down)
    embedded_wide = embedded.astype(jnp.float32)
    state = embedded
    for layer in range(len(cross_down)):
        if layer > 0:
            term = jnp.dot(state, cross_down[layer], preferred_element_type=jnp.float32)
            term = term.astype(jnp.bfloat16)
        low = lax.psum(term, "mp")
        high = (
            jnp.dot(low, cross_up[layer], preferred_element_type=jnp.float32)
            + cross_bias[layer][None, :]
        )
        state = (embedded_wide * high + state.astype(jnp.float32)).astype(jnp.bfloat16)
    return state


def solution(mesh):
    return jax.shard_map(
        per_device,
        mesh=mesh,
        in_specs=(
            P("batch", None),
            P(),
            P("batch", None, None),
            P(None, "mp", None),
            P(None, None, "mp"),
            P(None, "mp"),
        ),
        out_specs=P("batch", "mp"),
        check_vma=False,
    )
```

time: 725 us -> 488 us (0.67)
  Pallas kernels: 0 us -> 321 us
  blocking collectives: 288 us -> 0 us
  local copies, waits for them, and re-layouts: 255 us -> 16.6 us
  other arithmetic: 23.4 us -> 3.42 us
  matrix products: 49.2 us -> 31.8 us
  waiting for transfers between devices: 89.2 us -> 101 us
    pallas_call x0 -> x3, Pallas kernels: none -> 321 us  [the longest x1 204 us: exchange(): pl.pallas_call(functools.partial(exchange_kernel, sources, groups), out_s...]
    all_to_all x2 -> x0, blocking collectives: 288 us -> none  [the longest x1 191 us: per_device(): lax.all_to_all(looked, 'batch', split_axis=0, concat_axis=0, tiled=True)]
    gather x8 -> x0, local copies, waits for them, and re-layouts: 102 us -> none  [per_device(): jnp.take(tables[slot], wanted[slot].reshape(sources * share), axis=0)]
    another operation x9 -> x0, local copies, waits for them, and re-layouts: 90.5 us -> none  [per_device(): jnp.stack([jnp.take(tables[slot], wanted[slot].reshape(sources * share),...]
    all_to_all x3 -> x0, local copies, waits for them, and re-layouts: 29.7 us -> none  [the longest x2 21.7 us: per_device(): lax.all_to_all(lax.all_to_all(looked, 'batch', split_axis=0, concat_axis=...]
    select_n x8 -> x0, other arithmetic: 23.3 us -> none  [per_device(): jnp.take(tables[slot], wanted[slot].reshape(sources * share), axis=0)]
    dot_general x3 -> x1, matrix products: 23.4 us -> 5.93 us  [per_device(): term = jnp.dot(state, cross_down[layer], preferred_element_type=jnp.float32)]
    psum x2, waiting for transfers between devices: 89.2 us -> 101 us  [per_device(): low = lax.psum(term, 'mp')]
  transfers between devices with their start and end apart: 2 -> 2, of which waited for: 2 -> 2; matrix products, arithmetic and copies ran while one was open for 2% -> 0% of each run, Pallas kernels for 0% -> 0%
where the time goes in v1:
time: 488 us
  Pallas kernels  321 us (66%)
  waiting for transfers between devices  101 us (21%)
  matrix products  31.8 us (7%)
  local copies, waits for them, and re-layouts  16.6 us (3%)
  between operations  13.5 us (3%)
    pallas_call x1, Pallas kernels, exchange(): pl.pallas_call(functools.partial(exchange_kernel, sources, groups), out_s...  204 us
    psum x2, waiting for transfers between devices, per_device(): low = lax.psum(term, 'mp')  101 us
    pallas_call x1, Pallas kernels, gather(): pl.pallas_call(gather_kernel, out_shape=jax.ShapeDtypeStruct((sources, gr...  99.4 us
    dot_general x2, matrix products, per_device(): jnp.dot(low, cross_up[layer], preferred_element_type=jnp.float32)  25.9 us
    pallas_call x1, Pallas kernels, place(): pl.pallas_call(place_kernel, out_shape=(jax.ShapeDtypeStruct((groups * sh...  17.8 us
    unnamed x18, local copies, waits for them, and re-layouts  11.1 us
  transfers between devices with their start and end apart: 2, of which 2 were waited for; matrix products, arithmetic and copies ran while one was open for 0% of the time, Pallas kernels for 0%

profile of v1, /device:TPU:0, one launch (start us, length us, event | category | flops | bytes accessed | tf_op | source)
XLA Modules:
  0.0 487.7 jit_solution(15351311872679988425)
XLA Ops:
  6.5 0.0 copy-start
  6.5 0.0 all-reduce.3.cloned.1.call-start
  6.6 1.0 copy-done
  7.6 99.4 %lookup.1.src_ref = bf16[8,4,8,32,512]{4,3,2,1,0:T(8,128)(2,1)S(1)} custom-call(s32[8,4096]{1,0:T(8,128)S(1)} %bitcast.19, bf16[8,8192,128]{2,1,0:T(8,128)(2,1)} %table_ref.1), custom_call_target="tpu_custom_call" | custom-call | tf_op jit(solution)/shard_map/lookup/pallas_call | solution.py:44
  107.0 0.0 copy-start.2
  107.0 3.4 copy-done.2
  110.4 0.0 copy-start.7
  110.4 203.9 %exchange.1.x_ref = bf16[8,4,8,32,512]{4,3,2,1,0:T(8,128)(2,1)} custom-call(bf16[8,4,8,32,512]{4,3,2,1,0:T(8,128)(2,1)} %copy-done.2), custom_call_target="tpu_custom_call" | custom-call | tf_op jit(solution)/shard_map/exchange/pallas_call | solution.py:109
  314.2 0.0 copy-done.7
  314.2 0.1 iota_compare_fusion
  314.3 3.3 and_convert_fusion
  317.6 5.5 %reshape.44.placing_ref = bf16[1024,1024]{1,0:T(8,128)(2,1)S(1)} reshape(bf16[64,16,16,64]{3,2,1,0:T(8,128)(2,1)} %and_convert_fusion) | data formatting | bytes 4194304 | tf_op jit(solution)/shard_map/convert_element_type | solution.py:190
  323.1 0.0 copy-start.3
  323.1 2.2 copy-done.3
  325.3 0.0 copy-start.6
  325.3 17.8 %place.1 = (bf16[2048,2048]{1,0:T(8,128)(2,1)}, bf16[2048,512]{1,0:T(8,128)(2,1)S(1)}) custom-call(bf16[8,4,8,32,512]{4,3,2,1,0:T(8,128)(2,1)} %exchange.1.x_ref, bf16[1024,1024]{1,0:T(8,128)(2,1)S(1)} %reshape.44.placing_ref, bf16[2,2048,512]{2,1,0:T(8,128)(2,1)S(1)} %copy-done.3), custom_call_target="tpu_custom_call" | custom-call | tf_op jit(solution)/shard_map/place/pallas_call | solution.py:151
  343.1 0.0 copy-start.5
  343.1 1.3 copy-done.5
  344.4 0.0 all-reduce.3.cloned.1.call-update
  344.4 0.0 all-reduce.5.cloned.1.call-start
  344.5 0.0 copy-done.6
  344.5 49.7 %all-reduce.3.cloned.1.call-done = bf16[2048,512]{1,0:T(8,128)(2,1)} async-done(((bf16[2048,512]{1,0:T(8,128)(2,1)}), bf16[2048,512]{1,0:T(8,128)(2,1)}) %all-reduce.3.cloned.1.call-update) | async-done | bytes 2097168 | tf_op jit(solution)/shard_map/psum | solution.py:199
  394.2 0.0 copy-start.4
  394.2 9.9 %fusion.2 = bf16[2048,2048]{1,0:T(8,128)(2,1)S(1)} fusion(bf16[2048,2048]{1,0:T(8,128)(2,1)} %get-tuple-element.7, f32[2048]{0:T(1024)S(1)} %bitcast.21, bf16[2048,512]{1,0:T(8,128)(2,1)} %all-reduce.3.cloned.1.call-done, bf16[2,512,2048]{2,1,0:T(8,128)(2,1)} %param.10), kind=kOutput, calls=%fused_computation.4 | convolution fusion | flops 4315938816 | bytes 20979712 | tf_op jit(solution)/shard_map/dot_general | solution.py:201
  404.1 0.0 copy-start.8
  404.1 3.2 copy-done.8
  407.3 0.0 copy-done.4
  407.3 5.9 %convolution_convert_fusion = bf16[2048,512]{1,0:T(8,128)(2,1)} fusion(bf16[2048,2048]{1,0:T(8,128)(2,1)S(1)} %fusion.2, bf16[2,2048,512]{2,1,0:T(8,128)(2,1)S(1)} %copy-done.4), kind=kOutput, calls=%fused_computation.6 | convolution fusion | flops 4296015872 | bytes 12582912 | tf_op jit(solution)/shard_map/dot_general | solution.py:197
  413.3 0.0 all-reduce.5.cloned.1.call-update
  413.3 51.6 %all-reduce.5.cloned.1.call-done = bf16[2048,512]{1,0:T(8,128)(2,1)} async-done(((bf16[2048,512]{1,0:T(8,128)(2,1)}), bf16[2048,512]{1,0:T(8,128)(2,1)}) %all-reduce.5.cloned.1.call-update) | async-done | bytes 2097168 | tf_op jit(solution)/shard_map/psum | solution.py:199
  464.9 0.0 copy-start.1
  464.9 15.9 %fusion.1 = bf16[2048,2048]{1,0:T(8,128)(2,1)} fusion(bf16[2048,2048]{1,0:T(8,128)(2,1)} %get-tuple-element.7, bf16[2048,2048]{1,0:T(8,128)(2,1)} %copy-done.8, f32[2048]{0:T(1024)S(1)} %bitcast.20, bf16[2048,512]{1,0:T(8,128)(2,1)} %all-reduce.5.cloned.1.call-done, bf16[2,512,2048]{2,1,0:T(8,128)(2,1)} %param.10), kind=kOutput, calls=%fused_computation.3 | convolution fusion | flops 4320133120 | bytes 29368320 | tf_op jit(solution)/shard_map/dot_general | solution.py:201
  480.8 0.0 copy-done.1
  (3 shorter events, 0.0 us)
Async XLA Ops:
  6.5 1.0 copy-start
  6.5 387.6 %all-reduce.3.cloned.1.call-start = ((), (), s32[]{:S(2)}) async-start(), calls=%async_computation | async-start | bytes 4194304 | tf_op jit(solution)/shard_map/psum | solution.py:199
  107.0 3.4 copy-start.2
  110.4 203.9 %copy-start.7 = (s32[64]{0:T(128)S(1)}, s32[64]{0:T(128)}, u32[]{:S(2)}) copy-start(s32[64]{0:T(128)} %param.7) | copy-start | bytes 772
  323.1 2.2 copy-start.3
  325.3 19.2 %copy-start.6 = (f32[2,2048]{1,0:T(2,128)S(1)}, f32[2,2048]{1,0:T(2,128)}, u32[]{:S(2)}) copy-start(f32[2,2048]{1,0:T(2,128)} %param.11) | copy-start | bytes 49156
  343.1 1.3 copy-start.5
  344.4 120.5 %all-reduce.5.cloned.1.call-start = ((), (), s32[]{:S(2)}) async-start(), calls=%async_computation.1 | async-start | bytes 4194304 | tf_op jit(solution)/shard_map/psum | solution.py:199
  394.2 13.2 %copy-start.4 = (bf16[2,2048,512]{2,1,0:T(8,128)(2,1)S(1)}, bf16[2,2048,512]{2,1,0:T(8,128)(2,1)}, u32[]{:S(2)}) copy-start(bf16[2,2048,512]{2,1,0:T(8,128)(2,1)} %down_ref.1) | copy-start | bytes 12582916
  404.1 3.2 copy-start.8
  464.9 15.9 %copy-start.1 = (s32[8,16384]{1,0:T(8,128)S(1)}, s32[8,16384]{1,0:T(8,128)}, u32[]{:S(2)}) copy-start(s32[8,16384]{1,0:T(8,128)} %param.6) | copy-start | bytes 1572868
Sparse Core Ops, SparseCore 0:
  344.6 49.5 all-reduce.2
  413.4 51.4 all-reduce.4

commit v2 on v1

--- a/solution.py
+++ b/solution.py
@@ -121,9 +121,15 @@
     )(sent)
 
 
-def place_kernel(x_ref, placing_ref, down_ref, emb_ref, term_ref, total):
+def place_kernel(x_ref, column_ref, down_ref, emb_ref, term_ref, placing_ref, total):
     sources, _, slots, group, share = x_ref.shape
-    j = pl.program_id(1)
+    i, j = pl.program_id(0), pl.program_id(1)
+
+    @pl.when((i == 0) & (j == 0))
+    def _():
+        columns = lax.broadcasted_iota(jnp.int32, placing_ref.shape, 1)
+        placing_ref[...] = jnp.where(column_ref[...] == columns, 1.0, 0.0).astype(jnp.bfloat16)
+
     x = x_ref[...].reshape(sources * slots * group, share)
     emb = lax.dot_general(
         x, placing_ref[...], (((0,), (0,)), ((), ())), preferred_element_type=jnp.float32
@@ -144,7 +150,7 @@
         term_ref[...] = total[...].astype(jnp.bfloat16)
 
 
-def place(received, placing, cross_down):
+def place(received, column, cross_down):
     sources, groups, slots, emb_local, share = received.shape
     _, width, rank = cross_down.shape
     cols = sources * slots * GROUP
@@ -157,17 +163,115 @@
         grid=(groups, emb_local // GROUP),
         in_specs=[
             pl.BlockSpec((sources, 1, slots, GROUP, share), lambda i, j: (0, i, 0, j, 0)),
-            pl.BlockSpec((cols, cols), lambda i, j: (0, 0)),
+            pl.BlockSpec((cols, 1), lambda i, j: (0, 0)),
             pl.BlockSpec((1, cols, rank), lambda i, j: (0, j, 0)),
         ],
         out_specs=(
             pl.BlockSpec((share, cols), lambda i, j: (i, j)),
             pl.BlockSpec((share, rank), lambda i, j: (i, 0)),
         ),
-        scratch_shapes=[pltpu.VMEM((share, rank), jnp.float32)],
+        scratch_shapes=[
+            pltpu.VMEM((cols, cols), jnp.bfloat16),
+            pltpu.VMEM((share, rank), jnp.float32),
+        ],
         compiler_params=pltpu.CompilerParams(vmem_limit_bytes=40 * 2**20),
         name="place",
-    )(received, placing, cross_down)
+    )(received, column, cross_down)
+
+
+PIECES = 4
+
+
+def reduce_kernel(groups, term_ref, low_ref, near_in, held, far_in, *sems):
+    b, m = lax.axis_index("batch"), lax.axis_index("mp")
+    near_send, near_recv, far_send, far_recv, back_send, back_recv = sems
+    near = (b, partner(m, 1, groups))
+    far = [(b, partner(m, 1 << (s + 1), groups)) for s in range(far_in.shape[0])]
+    half = term_ref.shape[0] // 2
+    piece = half // PIECES
+    core = m % 2
+
+    def rows(who, k):
+        return pl.ds(pl.multiple_of(who * half + k * piece, piece), piece)
+
+    barrier = pltpu.get_barrier_semaphore()
+    for peer in [near] + far:
+        pl.semaphore_signal(barrier, inc=1, device_id=peer, device_id_type=MESH)
+    pl.semaphore_wait(barrier, 1 + len(far))
+
+    def send(src, dst, send_sem, recv_sem, peer):
+        copy = pltpu.make_async_remote_copy(
+            src_ref=src,
+            dst_ref=dst,
+            send_sem=send_sem,
+            recv_sem=recv_sem,
+            device_id=peer,
+            device_id_type=MESH,
+        )
+        copy.start()
+        return copy
+
+    sent = []
+    going = [
+        send(term_ref.at[rows(1 - core, k)], near_in.at[k], near_send.at[k], near_recv.at[k], near)
+        for k in range(PIECES)
+    ]
+    for s in range(len(far) + 1):
+        arriving, going = going, []
+        for k in range(PIECES):
+            arriving[k].wait_recv()
+            if s == 0:
+                mine, other = term_ref[rows(core, k)], near_in[k]
+            else:
+                mine, other = held[s - 1, k], far_in[s - 1, k]
+            total = (mine.astype(jnp.float32) + other.astype(jnp.float32)).astype(jnp.bfloat16)
+            if s < len(far):
+                held[s, k] = total
+                going.append(
+                    send(
+                        held.at[s, k], far_in.at[s, k], far_send.at[s, k], far_recv.at[s, k], far[s]
+                    )
+                )
+            else:
+                place = rows(core, k)
+                low_ref[place] = total
+                going.append(
+                    send(low_ref.at[place], low_ref.at[place], back_send.at[k], back_recv.at[k], near)
+                )
+        sent += arriving
+    for copy in going:
+        copy.wait_recv()
+    for copy in sent + going:
+        copy.wait_send()
+
+
+def reduce_over_mp(term):
+    groups = lax.axis_size("mp")
+    stages = groups.bit_length() - 2
+    rows, rank = term.shape
+    block = (PIECES, rows // 2 // PIECES, rank)
+    dma = pltpu.SemaphoreType.DMA
+    return pl.pallas_call(
+        functools.partial(reduce_kernel, groups),
+        out_shape=jax.ShapeDtypeStruct(term.shape, term.dtype),
+        in_specs=[pl.BlockSpec(memory_space=pltpu.VMEM)],
+        out_specs=pl.BlockSpec(memory_space=pltpu.VMEM),
+        scratch_shapes=[
+            pltpu.VMEM(block, term.dtype),
+            pltpu.VMEM((stages,) + block, term.dtype),
+            pltpu.VMEM((stages,) + block, term.dtype),
+            dma((PIECES,)),
+            dma((PIECES,)),
+            dma((stages, PIECES)),
+            dma((stages, PIECES)),
+            dma((PIECES,)),
+            dma((PIECES,)),
+        ],
+        compiler_params=pltpu.CompilerParams(
+            collective_id=1, has_side_effects=True, vmem_limit_bytes=24 * 2**20
+        ),
+        name="reduce",
+    )(term)
 
 
 def per_device(lookup_ids, table_feature, tables, cross_down, cross_up, cross_bias):
@@ -182,21 +286,15 @@
     wanted = lax.dynamic_slice_in_dim(by_owner, start, share, 2)
     wanted = wanted.reshape(slots_local, sources * share)
     received = exchange(gather(wanted, tables, sources, groups, share))
-    fits = table_feature[:, None] == jnp.arange(feats, dtype=jnp.int32)[None, :]
-    same = jnp.arange(GROUP)[:, None] == jnp.arange(GROUP)[None, :]
-    placing = (
-        (fits[:, None, None, :] & same[None, :, :, None])
-        .reshape(feats * GROUP, GROUP * feats)
-        .astype(jnp.bfloat16)
-    )
-    embedded, term = place(received, placing, cross_down)
+    column = (table_feature[:, None] + feats * jnp.arange(GROUP)[None, :]).reshape(-1, 1)
+    embedded, term = place(received, column, cross_down)
     embedded_wide = embedded.astype(jnp.float32)
     state = embedded
     for layer in range(len(cross_down)):
         if layer > 0:
             term = jnp.dot(state, cross_down[layer], preferred_element_type=jnp.float32)
             term = term.astype(jnp.bfloat16)
-        low = lax.psum(term, "mp")
+        low = reduce_over_mp(term)
         high = (
             jnp.dot(low, cross_up[layer], preferred_element_type=jnp.float32)
             + cross_bias[layer][None, :]

time: 488 us -> 417 us (0.85)
  waiting for transfers between devices: 101 us -> 0 us
  Pallas kernels: 321 us -> 378 us
  between operations: 13.5 us -> 0.1 us
  local copies, waits for them, and re-layouts: 16.6 us -> 7.74 us
    psum x2 -> x0, waiting for transfers between devices: 101 us -> none  [per_device(): low = lax.psum(term, 'mp')]
    pallas_call x0 -> x2, Pallas kernels: none -> 56.4 us  [reduce_over_mp(): pl.pallas_call(functools.partial(reduce_kernel, groups), out_shape=jax.Sh...]
    convert_element_type x1 -> x0, local copies, waits for them, and re-layouts: 5.47 us -> none  [per_device(): placing = (fits[:, None, None, :] & same[None, :, :, None]).reshape(feats...]
    unnamed x18 -> x12, local copies, waits for them, and re-layouts: 11.1 us -> 6.63 us
  transfers between devices with their start and end apart: 2 -> 0, of which waited for: 2 -> 0; matrix products, arithmetic and copies ran while one was open for 0% -> 0% of each run, Pallas kernels for 0% -> 0%
where the time goes in v2:
time: 417 us; the launch traced here: 416 us
  Pallas kernels  378 us (91%)
  matrix products  29.6 us (7%)
  local copies, waits for them, and re-layouts  7.74 us (2%)
    pallas_call x1, Pallas kernels, exchange(): pl.pallas_call(functools.partial(exchange_kernel, sources, groups), out_s...  204 us
    pallas_call x1, Pallas kernels, gather(): pl.pallas_call(gather_kernel, out_shape=jax.ShapeDtypeStruct((sources, gr...  99.4 us
    pallas_call x2, Pallas kernels, reduce_over_mp(): pl.pallas_call(functools.partial(reduce_kernel, groups), out_shape=jax.Sh...  56.4 us
    dot_general x2, matrix products, per_device(): jnp.dot(low, cross_up[layer], preferred_element_type=jnp.float32)  21.5 us
    pallas_call x1, Pallas kernels, place(): pl.pallas_call(place_kernel, out_shape=(jax.ShapeDtypeStruct((groups * sh...  18.4 us

profile of v2, /device:TPU:0, one launch (start us, length us, event | category | flops | bytes accessed | tf_op | source)
XLA Modules:
  0.0 416.2 jit_solution(3842291374202485196)
XLA Ops:
  0.0 0.0 copy-start
  0.0 1.0 copy-done
  1.0 0.8 fusion.9
  1.9 0.7 broadcast_add_fusion
  2.6 0.3 add.65.column_ref
  2.9 99.4 %lookup.1.src_ref = bf16[8,4,8,32,512]{4,3,2,1,0:T(8,128)(2,1)S(1)} custom-call(s32[8,4096]{1,0:T(8,128)S(1)} %bitcast.17, bf16[8,8192,128]{2,1,0:T(8,128)(2,1)} %table_ref.1), custom_call_target="tpu_custom_call" | custom-call | tf_op jit(solution)/shard_map/lookup/pallas_call | solution.py:44
  102.3 0.0 copy-start.2
  102.3 3.4 copy-done.2
  105.7 203.8 %exchange.1.x_ref = bf16[8,4,8,32,512]{4,3,2,1,0:T(8,128)(2,1)} custom-call(bf16[8,4,8,32,512]{4,3,2,1,0:T(8,128)(2,1)} %copy-done.2), custom_call_target="tpu_custom_call" | custom-call | tf_op jit(solution)/shard_map/exchange/pallas_call | solution.py:109
  309.5 0.0 copy-start.3
  309.5 2.2 copy-done.3
  311.7 0.0 copy-start.5
  311.7 18.4 %place.1 = (bf16[2048,2048]{1,0:T(8,128)(2,1)}, bf16[2048,512]{1,0:T(8,128)(2,1)S(1)}) custom-call(bf16[8,4,8,32,512]{4,3,2,1,0:T(8,128)(2,1)} %exchange.1.x_ref, s32[1024,1]{1,0:T(8,128)S(1)} %add.65.column_ref, bf16[2,2048,512]{2,1,0:T(8,128)(2,1)S(1)} %copy-done.3), custom_call_target="tpu_custom_call" | custom-call | tf_op jit(solution)/shard_map/place/pallas_call | solution.py:157
  330.2 28.0 %reduce.2 = bf16[2048,512]{1,0:T(8,128)(2,1)S(1)} custom-call(bf16[2048,512]{1,0:T(8,128)(2,1)S(1)} %get-tuple-element.8.term_ref), custom_call_target="tpu_custom_call" | custom-call | tf_op jit(solution)/shard_map/reduce/pallas_call | solution.py:254
  358.2 0.0 copy-done.5
  358.2 0.0 copy-start.4
  358.2 10.0 %fusion.2 = bf16[2048,2048]{1,0:T(8,128)(2,1)} fusion(bf16[2048,2048]{1,0:T(8,128)(2,1)} %get-tuple-element.7, f32[2048]{0:T(1024)S(1)} %bitcast.19, bf16[2048,512]{1,0:T(8,128)(2,1)S(1)} %reduce.2, bf16[2,512,2048]{2,1,0:T(8,128)(2,1)S(1)} %copy-done.5), kind=kOutput, calls=%fused_computation.4 | convolution fusion | flops 4315938816 | bytes 20979712 | tf_op jit(solution)/shard_map/dot_general | solution.py:299
  368.2 0.0 copy-done.4
  368.2 8.1 %convolution_convert_fusion.term_ref = bf16[2048,512]{1,0:T(8,128)(2,1)S(1)} fusion(bf16[2048,2048]{1,0:T(8,128)(2,1)} %fusion.2, bf16[2,2048,512]{2,1,0:T(8,128)(2,1)S(1)} %copy-done.4), kind=kOutput, calls=%fused_computation.5 | convolution fusion | flops 4296015872 | bytes 12582912 | tf_op jit(solution)/shard_map/dot_general | solution.py:295
  376.3 28.4 %reduce.3 = bf16[2048,512]{1,0:T(8,128)(2,1)S(1)} custom-call(bf16[2048,512]{1,0:T(8,128)(2,1)S(1)} %convolution_convert_fusion.term_ref), custom_call_target="tpu_custom_call" | custom-call | tf_op jit(solution)/shard_map/reduce/pallas_call | solution.py:254
  404.8 0.0 copy-start.1
  404.8 11.5 %fusion.1 = bf16[2048,2048]{1,0:T(8,128)(2,1)} fusion(bf16[2048,2048]{1,0:T(8,128)(2,1)} %get-tuple-element.7, bf16[2048,2048]{1,0:T(8,128)(2,1)} %fusion.2, f32[2048]{0:T(1024)S(1)} %bitcast.18, bf16[2048,512]{1,0:T(8,128)(2,1)S(1)} %reduce.3, bf16[2,512,2048]{2,1,0:T(8,128)(2,1)} %param.10), kind=kOutput, calls=%fused_computation.3 | convolution fusion | flops 4320133120 | bytes 29368320 | tf_op jit(solution)/shard_map/dot_general | solution.py:299
  416.2 0.0 copy-done.1
  (2 shorter events, 0.0 us)
Async XLA Ops:
  0.0 1.0 copy-start
  102.3 3.4 copy-start.2
  309.5 2.2 copy-start.3
  311.7 46.5 %copy-start.5 = (bf16[2,512,2048]{2,1,0:T(8,128)(2,1)S(1)}, bf16[2,512,2048]{2,1,0:T(8,128)(2,1)}, u32[]{:S(2)}) copy-start(bf16[2,512,2048]{2,1,0:T(8,128)(2,1)} %param.10) | copy-start | bytes 12582916
  358.2 10.0 %copy-start.4 = (bf16[2,2048,512]{2,1,0:T(8,128)(2,1)S(1)}, bf16[2,2048,512]{2,1,0:T(8,128)(2,1)}, u32[]{:S(2)}) copy-start(bf16[2,2048,512]{2,1,0:T(8,128)(2,1)} %down_ref.1) | copy-start | bytes 12582916
  404.8 11.5 %copy-start.1 = (s32[8,16384]{1,0:T(8,128)S(1)}, s32[8,16384]{1,0:T(8,128)}, u32[]{:S(2)}) copy-start(s32[8,16384]{1,0:T(8,128)} %param.6) | copy-start | bytes 1572868

commit v3 on v2

--- a/solution.py
+++ b/solution.py
@@ -29,8 +29,9 @@
         @pl.loop(0, share // unroll)
         def _(i):
             base = pl.multiple_of(i * unroll, unroll)
+            first = (slot * sources + dest) * share + base
             for k in range(unroll):
-                at = ids_ref[slot, dest * share + base + k]
+                at = ids_ref[first + k]
                 rows[pl.ds(base + k, 1), :] = wide[pl.ds(at, 1), :]
 
         turned = rows[...].T.astype(jnp.bfloat16)
@@ -284,7 +285,7 @@
     start = lax.axis_index("mp") * share
     by_owner = lookup_ids.reshape(slots_local, sources, examples_local)
     wanted = lax.dynamic_slice_in_dim(by_owner, start, share, 2)
-    wanted = wanted.reshape(slots_local, sources * share)
+    wanted = wanted.reshape(slots_local * sources * share)
     received = exchange(gather(wanted, tables, sources, groups, share))
     column = (table_feature[:, None] + feats * jnp.arange(GROUP)[None, :]).reshape(-1, 1)
     embedded, term = place(received, column, cross_down)

time: 417 us -> 363 us (0.87)
  Pallas kernels: 378 us -> 325 us
    pallas_call x1, Pallas kernels: 99.4 us -> 46 us  [gather(): pl.pallas_call(gather_kernel, out_shape=jax.ShapeDtypeStruct((sources, gr...]
where the time goes in v3:
time: 363 us
  Pallas kernels  325 us (90%)
  matrix products  29.4 us (8%)
  local copies, waits for them, and re-layouts  7.86 us (2%)
    pallas_call x1, Pallas kernels, exchange(): pl.pallas_call(functools.partial(exchange_kernel, sources, groups), out_s...  204 us
    pallas_call x2, Pallas kernels, reduce_over_mp(): pl.pallas_call(functools.partial(reduce_kernel, groups), out_shape=jax.Sh...  56.4 us
    pallas_call x1, Pallas kernels, gather(): pl.pallas_call(gather_kernel, out_shape=jax.ShapeDtypeStruct((sources, gr...  46 us
    dot_general x2, matrix products, per_device(): jnp.dot(low, cross_up[layer], preferred_element_type=jnp.float32)  21.3 us
    pallas_call x1, Pallas kernels, place(): pl.pallas_call(place_kernel, out_shape=(jax.ShapeDtypeStruct((groups * sh...  18.4 us
    dot_general x1, matrix products, per_device(): term = jnp.dot(state, cross_down[layer], preferred_element_type=jnp.float32)  8.11 us

profile of v3, /device:TPU:0, one launch (start us, length us, event | category | flops | bytes accessed | tf_op | source)
XLA Modules:
  0.0 362.8 jit_solution(10604554340199990801)
XLA Ops:
  0.0 0.0 copy-start
  0.0 1.0 copy-done
  1.0 0.8 fusion.9
  1.9 0.7 broadcast_add_fusion
  2.6 0.1 copy.12
  2.7 0.3 add.65.column_ref
  3.0 46.0 %lookup.1.src_ref = bf16[8,4,8,32,512]{4,3,2,1,0:T(8,128)(2,1)S(1)} custom-call(s32[32768]{0:T(1024)S(1)} %bitcast.20, bf16[8,8192,128]{2,1,0:T(8,128)(2,1)} %table_ref.1), custom_call_target="tpu_custom_call" | custom-call | tf_op jit(solution)/shard_map/lookup/pallas_call | solution.py:45
  49.0 0.0 copy-start.2
  49.0 3.4 copy-done.2
  52.4 203.8 %exchange.1.x_ref = bf16[8,4,8,32,512]{4,3,2,1,0:T(8,128)(2,1)} custom-call(bf16[8,4,8,32,512]{4,3,2,1,0:T(8,128)(2,1)} %copy-done.2), custom_call_target="tpu_custom_call" | custom-call | tf_op jit(solution)/shard_map/exchange/pallas_call | solution.py:110
  256.3 0.0 copy-start.3
  256.3 2.2 copy-done.3
  258.5 0.0 copy-start.5
  258.5 18.4 %place.1 = (bf16[2048,2048]{1,0:T(8,128)(2,1)}, bf16[2048,512]{1,0:T(8,128)(2,1)S(1)}) custom-call(bf16[8,4,8,32,512]{4,3,2,1,0:T(8,128)(2,1)} %exchange.1.x_ref, s32[1024,1]{1,0:T(8,128)S(1)} %add.65.column_ref, bf16[2,2048,512]{2,1,0:T(8,128)(2,1)S(1)} %copy-done.3), custom_call_target="tpu_custom_call" | custom-call | tf_op jit(solution)/shard_map/place/pallas_call | solution.py:158
  276.9 28.0 %reduce.2 = bf16[2048,512]{1,0:T(8,128)(2,1)S(1)} custom-call(bf16[2048,512]{1,0:T(8,128)(2,1)S(1)} %get-tuple-element.8.term_ref), custom_call_target="tpu_custom_call" | custom-call | tf_op jit(solution)/shard_map/reduce/pallas_call | solution.py:255
  304.9 0.0 copy-done.5
  304.9 0.0 copy-start.4
  304.9 10.1 %fusion.2 = bf16[2048,2048]{1,0:T(8,128)(2,1)} fusion(bf16[2048,2048]{1,0:T(8,128)(2,1)} %get-tuple-element.7, f32[2048]{0:T(1024)S(1)} %bitcast.23, bf16[2048,512]{1,0:T(8,128)(2,1)S(1)} %reduce.2, bf16[2,512,2048]{2,1,0:T(8,128)(2,1)S(1)} %copy-done.5), kind=kOutput, calls=%fused_computation.4 | convolution fusion | flops 4315938816 | bytes 20979712 | tf_op jit(solution)/shard_map/dot_general | solution.py:300
  315.0 0.0 copy-done.4
  315.0 8.1 %convolution_convert_fusion.term_ref = bf16[2048,512]{1,0:T(8,128)(2,1)S(1)} fusion(bf16[2048,2048]{1,0:T(8,128)(2,1)} %fusion.2, bf16[2,2048,512]{2,1,0:T(8,128)(2,1)S(1)} %copy-done.4), kind=kOutput, calls=%fused_computation.5 | convolution fusion | flops 4296015872 | bytes 12582912 | tf_op jit(solution)/shard_map/dot_general | solution.py:296
  323.1 28.4 %reduce.3 = bf16[2048,512]{1,0:T(8,128)(2,1)S(1)} custom-call(bf16[2048,512]{1,0:T(8,128)(2,1)S(1)} %convolution_convert_fusion.term_ref), custom_call_target="tpu_custom_call" | custom-call | tf_op jit(solution)/shard_map/reduce/pallas_call | solution.py:255
  351.5 0.0 copy-start.1
  351.5 11.3 %fusion.1 = bf16[2048,2048]{1,0:T(8,128)(2,1)} fusion(bf16[2048,2048]{1,0:T(8,128)(2,1)} %get-tuple-element.7, bf16[2048,2048]{1,0:T(8,128)(2,1)} %fusion.2, f32[2048]{0:T(1024)S(1)} %bitcast.22, bf16[2048,512]{1,0:T(8,128)(2,1)S(1)} %reduce.3, bf16[2,512,2048]{2,1,0:T(8,128)(2,1)S(1)} %copy-done.5), kind=kOutput, calls=%fused_computation.3 | convolution fusion | flops 4320133120 | bytes 29368320 | tf_op jit(solution)/shard_map/dot_general | solution.py:300
  362.8 0.0 copy-done.1
  (3 shorter events, 0.0 us)
Async XLA Ops:
  0.0 1.0 copy-start
  49.0 3.4 copy-start.2
  256.3 2.2 copy-start.3
  258.5 46.4 %copy-start.5 = (bf16[2,512,2048]{2,1,0:T(8,128)(2,1)S(1)}, bf16[2,512,2048]{2,1,0:T(8,128)(2,1)}, u32[]{:S(2)}) copy-start(bf16[2,512,2048]{2,1,0:T(8,128)(2,1)} %param.10) | copy-start | bytes 12582916
  304.9 10.1 %copy-start.4 = (bf16[2,2048,512]{2,1,0:T(8,128)(2,1)S(1)}, bf16[2,2048,512]{2,1,0:T(8,128)(2,1)}, u32[]{:S(2)}) copy-start(bf16[2,2048,512]{2,1,0:T(8,128)(2,1)} %down_ref.1) | copy-start | bytes 12582916
  351.5 11.3 %copy-start.1 = (s32[8,16384]{1,0:T(8,128)S(1)}, s32[8,16384]{1,0:T(8,128)}, u32[]{:S(2)}) copy-start(s32[8,16384]{1,0:T(8,128)} %param.6) | copy-start | bytes 1572868
